TPU v7x, 32 devices: a whole 2x2x4 slice. The times are simulated.
32 devices in a mesh: rep: 4 (over x, core), fsdp: 8 (over z, y).
Axes of the slice: x: 2, y: 2, z: 4, core: 2. Of those that a mesh axis runs over, the one named last changes fastest.
Arguments:
- features: bfloat16 [4096, 1280], P(('rep', 'fsdp')), may hold values from -6 to 6
- cotangent: bfloat16 [4096, 1280], P(('rep', 'fsdp')), may hold values from -1 to 1
- clip_lengths: int32 [4, 8], P('rep'), may hold values from 96 to 128, as said below
- group_clips: int32 [4], P('rep'), may hold values from 6 to 8, as said below
- outer_attention: float32 [2, 1280, 5120], P(None, 'fsdp')
- outer_feedforward: float32 [2, 1280, 10240], P(None, 'fsdp')
- outer_vectors: float32 [2, 12, 1280], P(None, None, 'fsdp')
- moments_attention: float32 [4, 2, 1280, 5120], P('rep', None, 'fsdp')
- moments_feedforward: float32 [4, 2, 1280, 10240], P('rep', None, 'fsdp')
- moments_vectors: float32 [4, 2, 12, 1280], P('rep', None, None, 'fsdp')
Outputs:
- block_output: bfloat16 [4096, 1280], P(('rep', 'fsdp'))
- input_grad: float32 [4096, 1280], P(('rep', 'fsdp'))
- group_attention: float32 [4, 3, 1280, 5120], P('rep', None, 'fsdp')
- group_feedforward: float32 [4, 3, 1280, 10240], P('rep', None, 'fsdp')
- group_vectors: float32 [4, 3, 12, 1280], P('rep', None, None, 'fsdp')
- group_weights: float32 [4, 1280, 15372], P('rep', 'fsdp')
- next_attention: float32 [3, 1280, 5120], P(None, 'fsdp')
- next_feedforward: float32 [3, 1280, 10240], P(None, 'fsdp')
- next_vectors: float32 [3, 12, 1280], P(None, None, 'fsdp')
- copy_attention: bfloat16 [1280, 5120], P('fsdp')
- copy_feedforward: bfloat16 [1280, 10240], P('fsdp')
- copy_vectors: bfloat16 [12, 1280], P(None, 'fsdp')
Inputs may be any that keep to these rules, and one draw needn't show every extreme that they name: `clip_lengths`: some clip has exactly 128 valid tokens and some exactly 96. Group g holds clips in its slots 0 to group_clips[g] - 1 and none in the others; some group has all 8 and some 8 - 2.
All inputs are finite; a program needn't handle non-finite values.
Results may differ from a plain program's by a relative error of at most 0.012.
The roundings to bfloat16 on the way count: a program that leaves them out, or rounds other values in their place, can miss the bound.
Values may be sent and summed in bfloat16 or wider, within the bound.
A program may use at most 448 MiB of HBM per device.

v0:
```python
from functools import partial
import jax
import jax.numpy as jnp
from jax import lax
from jax.sharding import PartitionSpec as P

D = 1280
HEADS = 16
HD = 80
FF = 5120
STEP = 3
NORM_EPS = 1e-05
MASKED = -1e30
ADAM_RATE = 0.03
ADAM_DECAY = 0.1
ADAM_BETA = 0.5
ADAM_EPS = 1e-08
OUTER_RATE = 0.7
OUTER_MOMENTUM = 0.5


def contract_last(left, right):
    return lax.dot_general(
        left, right, (((1,), (1,)), ((), ())), preferred_element_type=jnp.float32
    )


def contract_rows(left, right):
    return lax.dot_general(
        left, right, (((0,), (0,)), ((), ())), preferred_element_type=jnp.float32
    )


def normalize(inputs, gain_row, shift_row):
    average = jnp.mean(inputs, axis=-1, keepdims=True)
    centered = inputs - average
    reciprocal = lax.rsqrt(jnp.mean(centered * centered, axis=-1, keepdims=True) + NORM_EPS)
    unit_rows = centered * reciprocal
    return (unit_rows * gain_row + shift_row, unit_rows, reciprocal)


def normalize_back(incoming, unit_rows, reciprocal, gain_row):
    scaled = incoming * gain_row
    centered = scaled - jnp.mean(scaled, axis=-1, keepdims=True)
    return reciprocal * (
        centered - unit_rows * jnp.mean(scaled * unit_rows, axis=-1, keepdims=True)
    )


def adamw_step(weight, gradient, moments, decay_rate):
    first_moment = ADAM_BETA * moments[0] + (1.0 - ADAM_BETA) * gradient
    second_moment = ADAM_BETA * moments[1] + (1.0 - ADAM_BETA) * gradient * gradient
    correction = 1.0 - ADAM_BETA**STEP
    direction = first_moment / correction / (jnp.sqrt(second_moment / correction) + ADAM_EPS)
    return (weight - ADAM_RATE * (direction + decay_rate * weight), first_moment, second_moment)


def outer_step(master, mean_delta, momentum_old):
    momentum = OUTER_MOMENTUM * momentum_old - mean_delta
    outer_next = master - OUTER_RATE * (OUTER_MOMENTUM * momentum - mean_delta)
    return jnp.stack([mean_delta, momentum, outer_next])


def shards(
    features,
    cotangent,
    clip_lengths,
    group_clips,
    outer_attention,
    outer_feedforward,
    outer_vectors,
    moments_attention,
    moments_feedforward,
    moments_vectors,
):
    tokens_here = features.shape[0]
    scale = HD ** (-0.5)
    clip_slot = lax.axis_index("fsdp")
    clip_length = lax.dynamic_index_in_dim(clip_lengths[0], clip_slot, keepdims=False)
    live_clip = clip_slot < group_clips[0]
    positions = jnp.arange(tokens_here, dtype=jnp.int32)
    key_valid = positions < clip_length
    row_valid = key_valid & live_clip
    masters = (outer_attention[0], outer_feedforward[0], outer_vectors[0])
    copies = (
        masters[0].astype(jnp.bfloat16),
        masters[1].astype(jnp.bfloat16),
        masters[2].astype(jnp.bfloat16),
    )
    full_attention, full_feedforward, full_vectors = (
        lax.all_gather(copies[0], "fsdp", axis=0, tiled=True),
        lax.all_gather(copies[1], "fsdp", axis=0, tiled=True),
        lax.all_gather(copies[2], "fsdp", axis=1, tiled=True),
    )
    vectors = full_vectors.astype(jnp.float32)
    inputs = features.astype(jnp.float32)
    normed_one, unit_one, scale_one = normalize(inputs, vectors[0], vectors[1])
    layer_one = normed_one.astype(jnp.bfloat16)
    qkv_bias = jnp.concatenate([vectors[2], jnp.zeros_like(vectors[2]), vectors[3]])
    projected = (
        jnp.dot(layer_one, full_attention[:, : 3 * D], preferred_element_type=jnp.float32)
        + qkv_bias
    ).astype(jnp.bfloat16)
    query_heads = projected[:, :D].reshape(tokens_here, HEADS, HD)
    key_heads = projected[:, D : 2 * D].reshape(tokens_here, HEADS, HD)
    value_heads = projected[:, 2 * D :].reshape(tokens_here, HEADS, HD)

    def score_block():
        raw_scores = (
            jnp.einsum("qhd,khd->hqk", query_heads, key_heads, preferred_element_type=jnp.float32)
            * scale
        )
        return jnp.where(key_valid[None, None, :], raw_scores, MASKED)

    scores = score_block()
    top_score = jnp.max(scores, axis=-1, keepdims=True)
    exponent = jnp.exp(scores - top_score)
    totals = jnp.sum(exponent, axis=-1, keepdims=True)
    attention_probs = exponent / totals
    log_totals = top_score + jnp.log(totals)
    attended = jnp.einsum(
        "hqk,khd->qhd",
        attention_probs.astype(jnp.bfloat16),
        value_heads,
        preferred_element_type=jnp.float32,
    )
    attended = attended.reshape(tokens_here, D).astype(jnp.bfloat16)
    attention_branch = contract_last(attended, full_attention[:, 3 * D :]) + vectors[4]
    middle = inputs + attention_branch
    normed_two, unit_two, scale_two = normalize(middle, vectors[5], vectors[6])
    layer_two = normed_two.astype(jnp.bfloat16)
    pre_activation = jnp.dot(
        layer_two, full_feedforward[:, :FF], preferred_element_type=jnp.float32
    ) + vectors[8:].reshape(FF)
    activation, gelu_backward = jax.vjp(partial(jax.nn.gelu, approximate=False), pre_activation)
    activation_low = activation.astype(jnp.bfloat16)
    feedforward_branch = contract_last(activation_low, full_feedforward[:, FF:]) + vectors[7]
    block_output = (middle + feedforward_branch).astype(jnp.bfloat16)
    back_attention, back_feedforward, back_vectors = (
        lax.all_gather(copies[0], "fsdp", axis=0, tiled=True),
        lax.all_gather(copies[1], "fsdp", axis=0, tiled=True),
        lax.all_gather(copies[2], "fsdp", axis=1, tiled=True),
    )
    gain_rows = back_vectors.astype(jnp.float32)
    upstream = cotangent.astype(jnp.float32) * row_valid[:, None].astype(jnp.float32)
    upstream_low = upstream.astype(jnp.bfloat16)
    grad_down_bias = jnp.sum(upstream_low, axis=0, dtype=jnp.float32)
    grad_activation = jnp.dot(
        upstream_low, back_feedforward[:, FF:], preferred_element_type=jnp.float32
    )
    grad_pre = gelu_backward(grad_activation)[0].astype(jnp.bfloat16)
    grad_up_bias = jnp.sum(grad_pre, axis=0, dtype=jnp.float32)
    grad_two = contract_last(grad_pre, back_feedforward[:, :FF])
    grad_gain_two = jnp.sum(grad_two * unit_two, axis=0)
    grad_shift_two = jnp.sum(grad_two, axis=0)
    grad_middle = upstream + normalize_back(grad_two, unit_two, scale_two, gain_rows[5])
    middle_low = grad_middle.astype(jnp.bfloat16)
    grad_out_bias = jnp.sum(middle_low, axis=0, dtype=jnp.float32)
    grad_attended = jnp.dot(
        middle_low, back_attention[:, 3 * D :], preferred_element_type=jnp.float32
    ).astype(jnp.bfloat16)
    grad_heads = grad_attended.reshape(tokens_here, HEADS, HD)
    attention_probs = jnp.exp(score_block() - log_totals)
    grad_probs = jnp.einsum(
        "qhd,khd->hqk", grad_heads, value_heads, preferred_element_type=jnp.float32
    )
    row_dot = jnp.sum(attention_probs * grad_probs, axis=-1, keepdims=True)
    grad_scores = (attention_probs * (grad_probs - row_dot)).astype(jnp.bfloat16)
    grad_queries = (
        jnp.einsum("hqk,khd->qhd", grad_scores, key_heads, preferred_element_type=jnp.float32)
        * scale
    ).reshape(tokens_here, D)
    grad_keys = (
        jnp.einsum("hqk,qhd->khd", grad_scores, query_heads, preferred_element_type=jnp.float32)
        * scale
    ).reshape(tokens_here, D)
    grad_values = jnp.einsum(
        "hqk,qhd->khd",
        attention_probs.astype(jnp.bfloat16),
        grad_heads,
        preferred_element_type=jnp.float32,
    ).reshape(tokens_here, D)
    grad_qkv = jnp.concatenate([grad_queries, grad_keys, grad_values], axis=1).astype(jnp.bfloat16)
    grad_query_bias = jnp.sum(grad_qkv[:, :D], axis=0, dtype=jnp.float32)
    grad_value_bias = jnp.sum(grad_qkv[:, 2 * D :], axis=0, dtype=jnp.float32)
    grad_one = contract_last(grad_qkv, back_attention[:, : 3 * D])
    grad_gain_one = jnp.sum(grad_one * unit_one, axis=0)
    grad_shift_one = jnp.sum(grad_one, axis=0)
    input_grad = grad_middle + normalize_back(grad_one, unit_one, scale_one, gain_rows[0])
    vector_rows = jnp.stack(
        [
            grad_gain_one,
            grad_shift_one,
            grad_query_bias,
            grad_value_bias,
            grad_out_bias,
            grad_gain_two,
            grad_shift_two,
            grad_down_bias,
        ]
    )
    grad_vectors = jnp.concatenate([vector_rows, grad_up_bias.reshape(4, D)], axis=0)
    owned_attention = lax.psum_scatter(
        jnp.concatenate(
            [contract_rows(layer_one, grad_qkv), contract_rows(middle_low, attended)], axis=1
        ),
        "fsdp",
        scatter_dimension=0,
        tiled=True,
    )
    owned_feedforward = lax.psum_scatter(
        jnp.concatenate(
            [contract_rows(layer_two, grad_pre), contract_rows(upstream_low, activation_low)],
            axis=1,
        ),
        "fsdp",
        scatter_dimension=0,
        tiled=True,
    )
    owned_vectors = lax.psum_scatter(grad_vectors, "fsdp", scatter_dimension=1, tiled=True)
    new_attention, first_attention, second_attention = adamw_step(
        masters[0], owned_attention, moments_attention[0], ADAM_DECAY
    )
    new_feedforward, first_feedforward, second_feedforward = adamw_step(
        masters[1], owned_feedforward, moments_feedforward[0], ADAM_DECAY
    )
    new_vectors, first_vectors, second_vectors = adamw_step(
        masters[2], owned_vectors, moments_vectors[0], 0.0
    )
    summed = (
        lax.psum_scatter(
            (new_attention - masters[0]).astype(jnp.bfloat16),
            "rep",
            scatter_dimension=1,
            tiled=True,
        ).astype(jnp.float32),
        lax.psum_scatter(
            (new_feedforward - masters[1]).astype(jnp.bfloat16),
            "rep",
            scatter_dimension=1,
            tiled=True,
        ).astype(jnp.float32),
        lax.psum_scatter(
            (new_vectors - masters[2]).astype(jnp.bfloat16), "rep", scatter_dimension=0, tiled=True
        ).astype(jnp.float32),
    )
    replicas = lax.axis_size("rep")
    replica_index = lax.axis_index("rep")
    attention_cols = 4 * D // replicas
    feedforward_cols = 2 * FF // replicas
    vector_count = 12 // replicas

    def owned_part(array, dim, count):
        return lax.dynamic_slice_in_dim(array, replica_index * count, count, dim)

    part_attention = outer_step(
        owned_part(masters[0], 1, attention_cols),
        summed[0] / replicas,
        owned_part(outer_attention[1], 1, attention_cols),
    )
    part_feedforward = outer_step(
        owned_part(masters[1], 1, feedforward_cols),
        summed[1] / replicas,
        owned_part(outer_feedforward[1], 1, feedforward_cols),
    )
    part_vectors = outer_step(
        owned_part(masters[2], 0, vector_count),
        summed[2] / replicas,
        owned_part(outer_vectors[1], 0, vector_count),
    )
    next_attention, next_feedforward, next_vectors = (
        lax.all_gather(part_attention, "rep", axis=2, tiled=True),
        lax.all_gather(part_feedforward, "rep", axis=2, tiled=True),
        lax.all_gather(part_vectors, "rep", axis=1, tiled=True),
    )
    copy_attention = next_attention[2].astype(jnp.bfloat16)
    copy_feedforward = next_feedforward[2].astype(jnp.bfloat16)
    copy_vectors = next_vectors[2].astype(jnp.bfloat16)
    group_attention = jnp.stack([owned_attention, first_attention, second_attention])[None]
    group_feedforward = jnp.stack([owned_feedforward, first_feedforward, second_feedforward])[None]
    group_vectors = jnp.stack([owned_vectors, first_vectors, second_vectors])[None]
    group_weights = jnp.concatenate([new_attention, new_feedforward, new_vectors.T], axis=1)[None]
    return (
        block_output,
        input_grad,
        group_attention,
        group_feedforward,
        group_vectors,
        group_weights,
        next_attention,
        next_feedforward,
        next_vectors,
        copy_attention,
        copy_feedforward,
        copy_vectors,
    )


def solution(mesh):
    in_specs = (
        P(("rep", "fsdp"), None),
        P(("rep", "fsdp"), None),
        P("rep", None),
        P("rep"),
        P(None, "fsdp", None),
        P(None, "fsdp", None),
        P(None, None, "fsdp"),
        P("rep", None, "fsdp", None),
        P("rep", None, "fsdp", None),
        P("rep", None, None, "fsdp"),
    )
    out_specs = (
        P(("rep", "fsdp"), None),
        P(("rep", "fsdp"), None),
        P("rep", None, "fsdp", None),
        P("rep", None, "fsdp", None),
        P("rep", None, None, "fsdp"),
        P("rep", "fsdp", None),
        P(None, "fsdp", None),
        P(None, "fsdp", None),
        P(None, None, "fsdp"),
        P("fsdp", None),
        P("fsdp", None),
        P(None, "fsdp"),
    )
    return jax.shard_map(shards, mesh=mesh, in_specs=in_specs, out_specs=out_specs, check_vma=False)
```

profile of v0, /device:TPU:0, one launch (start us, length us, event | category | flops | bytes accessed | tf_op | source)
XLA Modules:
  0.0 2351.6 jit_solution(7769149582330624274)
XLA Ops:
  17.1 33.6 %all-gather = bf16[8,160,12]{1,2,0:T(8,128)(2,1)S(1)} all-gather(bf16[1,160,12]{1,2,0:T(8,128)(2,1)S(1)} %copy.142), channel_id=1, replica_groups=mesh['rep'=4,'fsdp'=8] {'fsdp'}, dimensions={0}, use_global_device_ids=true | all-gather | bytes 34560 | tf_op jit(solution)/shard_map/all_gather | solution.py:93
  54.6 141.9 %all-gather.6.cloned.1.call-done = bf16[1280,5120]{1,0:T(8,128)(2,1)} async-done(((bf16[160,5120]{1,0:T(8,128)(2,1)}), bf16[1280,5120]{1,0:T(8,128)(2,1)}) %all-gather.6.cloned.1.call-update) | async-done | bytes 13107216 | tf_op jit(solution)/shard_map/all_gather | solution.py:91
  207.5 489.4 %all-gather.8.cloned.1.call-done = bf16[1280,10240]{1,0:T(8,128)(2,1)} async-done(((bf16[160,10240]{1,0:T(8,128)(2,1)}), bf16[1280,10240]{1,0:T(8,128)(2,1)}) %all-gather.8.cloned.1.call-update) | async-done | bytes 26214416 | tf_op jit(solution)/shard_map/all_gather | solution.py:92
  702.8 11.3 convert_reduce_fusion
  714.1 8.4 multiply_reduce_fusion.1
  736.2 9.2 pad_maximum_fusion.1
  745.6 13.1 fusion.115
  758.6 12.3 fusion.110
  770.9 34.1 %pad_maximum_fusion = f32[1280,10240]{1,0:T(8,128)} fusion(f32[1280,5120]{1,0:T(8,128)} %fusion.110, f32[1280,5120]{1,0:T(8,128)} %fusion.115), kind=kLoop, calls=%fused_computation | loop fusion | flops 13107200 | bytes 104857600 | tf_op jit(solution)/shard_map/concatenate | solution.py:212
  805.1 358.9 %reduce-scatter.7.cloned.1.call-done = f32[160,5120]{1,0:T(8,128)} async-done(((f32[1280,5120]{1,0:T(8,128)}), f32[160,5120]{1,0:T(8,128)}) %reduce-scatter.7.cloned.1.call-update) | async-done | bytes 3276816 | tf_op jit(solution)/shard_map/reduce_scatter | solution.py:203
  1164.0 9.6 fusion.29
  1173.7 811.0 %reduce-scatter.9.cloned.1.call-done = f32[160,10240]{1,0:T(8,128)} async-done(((f32[1280,10240]{1,0:T(8,128)}), f32[160,10240]{1,0:T(8,128)}) %reduce-scatter.9.cloned.1.call-update) | async-done | bytes 6553616 | tf_op jit(solution)/shard_map/reduce_scatter | solution.py:211
  1984.6 18.2 fusion.15
  2021.1 12.6 fusion.116
  2033.6 22.6 reduce-scatter.15.cloned.1.call-done
  2066.4 13.2 fusion.54
  2079.6 42.7 %reduce-scatter.11.cloned.1.call-done = f32[12,160]{0,1:T(8,128)} async-done(((f32[12,1280]{0,1:T(8,128)}), f32[12,160]{0,1:T(8,128)}) %reduce-scatter.11.cloned.1.call-update) | async-done | bytes 7696 | tf_op jit(solution)/shard_map/reduce_scatter | solution.py:220
  2127.6 12.0 all-reduce
  2146.3 8.3 maximum_bitcast_fusion.2
  2154.6 35.4 %all-gather.10.cloned.1.call-done = f32[3,160,5120]{2,1,0:T(8,128)} async-done(((f32[3,160,1280]{2,1,0:T(8,128)}), f32[3,160,5120]{2,1,0:T(8,128)}) %all-gather.10.cloned.1.call-update) | async-done | bytes 9830416 | tf_op jit(solution)/shard_map/all_gather | solution.py:272
  2193.4 19.0 maximum_bitcast_fusion
  2218.6 97.3 %all-gather.12.cloned.1.call-done = f32[3,160,10240]{2,1,0:T(8,128)} async-done(((f32[3,160,2560]{2,1,0:T(8,128)}), f32[3,160,10240]{2,1,0:T(8,128)}) %all-gather.12.cloned.1.call-update) | async-done | bytes 19660816 | tf_op jit(solution)/shard_map/all_gather | solution.py:273
  2320.8 8.8 copy.180
  2329.6 15.0 copy.181
  (158 shorter events, 97.5 us)
Async XLA Ops:
  7.2 44.4 %copy-start = (s32[1,8]{1,0:T(1,128)S(1)}, s32[1,8]{1,0:T(1,128)}, u32[]{:S(2)}) copy-start(s32[1,8]{1,0:T(1,128)} %param.12) | copy-start | bytes 100
  7.2 189.3 %all-gather.6.cloned.1.call-start = ((), (), s32[]{:S(2)}) async-start(), calls=%async_computation.5 | async-start | bytes 14745600 | tf_op jit(solution)/shard_map/all_gather | solution.py:91
  10.6 686.3 %all-gather.8.cloned.1.call-start = ((), (), s32[]{:S(2)}) async-start(), calls=%async_computation.6 | async-start | bytes 29491200 | tf_op jit(solution)/shard_map/all_gather | solution.py:92
  15.6 38.6 %copy-start.5 = (bf16[128,1280]{1,0:T(8,128)(2,1)S(1)}, bf16[128,1280]{1,0:T(8,128)(2,1)}, u32[]{:S(2)}) copy-start(bf16[128,1280]{1,0:T(8,128)(2,1)} %param.10) | copy-start | bytes 983044
  15.6 1148.4 %reduce-scatter.7.cloned.1.call-start = ((), (), s32[]{:S(2)}) async-start(), calls=%async_computation.7 | async-start | bytes 29491200 | tf_op jit(solution)/shard_map/reduce_scatter | solution.py:203
  17.1 184.8 %copy-start.9 = (f32[1,12,160]{1,2,0:T(8,128)}, f32[1,12,160]{1,2,0:T(8,128)S(1)}, u32[]{:S(2)}) copy-start(f32[1,12,160]{1,2,0:T(8,128)S(1)} %copy.171) | copy-start | bytes 23044
  207.2 538.3 %copy-start.4 = (f32[128,1280]{1,0:T(8,128)}, f32[128,1280]{1,0:T(8,128)S(1)}, u32[]{:S(2)}) copy-start(f32[128,1280]{1,0:T(8,128)S(1)} %get-tuple-element.138) | copy-start | bytes 1966084
  702.8 11.3 copy-start.21
  714.1 8.4 copy-start.8
  745.5 13.2 copy-start.15
  745.5 1239.1 %reduce-scatter.9.cloned.1.call-start = ((), (), s32[]{:S(2)}) async-start(), calls=%async_computation.8 | async-start | bytes 58982400 | tf_op jit(solution)/shard_map/reduce_scatter | solution.py:211
  745.5 13.1 copy-start.22
  805.0 1212.5 %reduce-scatter.13.cloned.1.call-start = ((), (), s32[]{:S(2)}) async-start(), calls=%async_computation.10 | async-start | bytes 2048000 | tf_op jit(solution)/shard_map/reduce_scatter | solution.py:231
  1173.6 882.6 %reduce-scatter.15.cloned.1.call-start = ((), (), s32[]{:S(2)}) async-start(), calls=%async_computation.12 | async-start | bytes 4096000 | tf_op jit(solution)/shard_map/reduce_scatter | solution.py:237
  2002.9 119.4 %reduce-scatter.11.cloned.1.call-start = ((), (), s32[]{:S(2)}) async-start(), calls=%async_computation.9 | async-start | bytes 737280 | tf_op jit(solution)/shard_map/reduce_scatter | solution.py:220
  2017.5 172.6 %all-gather.10.cloned.1.call-start = ((), (), s32[]{:S(2)}) async-start(), calls=%async_computation.11 | async-start | bytes 12288000 | tf_op jit(solution)/shard_map/all_gather | solution.py:272
  2021.0 294.8 %all-gather.12.cloned.1.call-start = ((), (), s32[]{:S(2)}) async-start(), calls=%async_computation.13 | async-start | bytes 24576000 | tf_op jit(solution)/shard_map/all_gather | solution.py:273
  2066.4 55.9 %copy-start.10 = (f32[1,12,160]{1,2,0:T(8,128)S(1)}, f32[1,12,160]{1,2,0:T(8,128)}, u32[]{:S(2)}) copy-start(f32[1,12,160]{1,2,0:T(8,128)} %copy-done.9) | copy-start | bytes 23044
  2066.4 79.9 %copy-start.2 = (f32[160,5120]{1,0:T(8,128)S(1)}, f32[160,5120]{1,0:T(8,128)}, u32[]{:S(2)}) copy-start(f32[160,5120]{1,0:T(8,128)} %reduce-scatter.7.cloned.1.call-done) | copy-start | bytes 9830404
  2145.7 9.0 copy-start.16
  2193.3 19.0 slice-start
  2193.3 19.0 slice-start.1
  2193.3 19.7 copy-start.3
  2329.6 15.0 copy-start.1
  (10 other events, 31.1 us)
Sparse Core Ops, SparseCore 0:
  10.8 185.6 all-gather.5
  198.6 498.2 all-gather.7
  745.6 418.3 reduce-scatter.6
  1167.8 816.8 reduce-scatter.8
  1987.6 27.6 reduce-scatter.12
  2017.7 38.5 reduce-scatter.14
  2059.5 62.7 reduce-scatter.10
  2123.9 66.1 all-gather.9
  2191.6 124.1 all-gather.11
where the time goes:
time: 2360 us; the launch traced here: 2350 us
  waiting for transfers between devices  2000 us (85%)
  other arithmetic  119 us (5%)
  matrix products  91.1 us (4%)
  local copies, waits for them, and re-layouts  74.3 us (3%)
  blocking collectives  51.4 us (2%)
    reduce_scatter x1, waiting for transfers between devices, shards(): lax.psum_scatter(jnp.concatenate([contract_rows(layer_two, grad_pre), con...  811 us
    all_gather x1, waiting for transfers between devices, shards(): lax.all_gather(copies[1], 'fsdp', axis=0, tiled=True)  489 us
    reduce_scatter x1, waiting for transfers between devices, shards(): lax.psum_scatter(jnp.concatenate([contract_rows(layer_one, grad_qkv), con...  359 us
    all_gather x1, waiting for transfers between devices, shards(): lax.all_gather(copies[0], 'fsdp', axis=0, tiled=True)  142 us
    all_gather x1, waiting for transfers between devices, shards(): lax.all_gather(part_feedforward, 'rep', axis=2, tiled=True)  97.3 us
  transfers between devices with their start and end apart: 9, of which 8 were waited for; matrix products, arithmetic and copies ran while one was open for 9% of the time, Pallas kernels for 0%

commit v1 on v0

--- a/solution.py
+++ b/solution.py
@@ -17,6 +17,18 @@
 ADAM_EPS = 1e-08
 OUTER_RATE = 0.7
 OUTER_MOMENTUM = 0.5
+
+
+def collect(x, axis, dim):
+    ways, here, step = (lax.axis_size(axis), lax.axis_index(axis), x.shape[dim])
+    line, have = (x, 1)
+    while have < ways:
+        line = jnp.concatenate(
+            [line, lax.ppermute(line, axis, [(d, (d - have) % ways) for d in range(ways)])],
+            axis=dim,
+        )
+        have = 2 * have
+    return jnp.roll(line, here * step, axis=dim)
 
 
 def contract_last(left, right):
@@ -88,7 +100,7 @@
         masters[2].astype(jnp.bfloat16),
     )
     full_attention, full_feedforward, full_vectors = (
-        lax.all_gather(copies[0], "fsdp", axis=0, tiled=True),
+        collect(copies[0], "fsdp", 0),
         lax.all_gather(copies[1], "fsdp", axis=0, tiled=True),
         lax.all_gather(copies[2], "fsdp", axis=1, tiled=True),
     )

time: 2360 us -> 2500 us (1.059)
  blocking collectives: 51.4 us -> 457 us
  waiting for transfers between devices: 2000 us -> 1690 us
  local copies, waits for them, and re-layouts: 74.3 us -> 99.7 us
    all_gather x1, waiting for transfers between devices: 489 us -> 0.02 us  [shards(): lax.all_gather(copies[1], 'fsdp', axis=0, tiled=True)]
    all_gather x1, blocking collectives: 33.6 us -> 440 us  [shards(): lax.all_gather(copies[2], 'fsdp', axis=1, tiled=True)]
    ppermute x0 -> x3, waiting for transfers between devices: none -> 233 us  [collect(): lax.ppermute(line, axis, [(d, (d - have) % ways) for d in range(ways)])]
    all_gather x1, waiting for transfers between devices: 142 us -> 89.5 us  [shards(): lax.all_gather(copies[0], 'fsdp', axis=0, tiled=True)]
  transfers between devices with their start and end apart: 9 -> 12, of which waited for: 8 -> 9; matrix products, arithmetic and copies ran while one was open for 9% -> 11% of each run, Pallas kernels for 0% -> 0%
where the time goes in v1:
time: 2500 us
  waiting for transfers between devices  1690 us (68%)
  blocking collectives  457 us (18%)
  other arithmetic  129 us (5%)
  local copies, waits for them, and re-layouts  99.7 us (4%)
  matrix products  93.4 us (4%)
    reduce_scatter x1, waiting for transfers between devices, shards(): lax.psum_scatter(jnp.concatenate([contract_rows(layer_two, grad_pre), con...  810 us
    all_gather x1, blocking collectives, shards(): lax.all_gather(copies[2], 'fsdp', axis=1, tiled=True)  440 us
    reduce_scatter x1, waiting for transfers between devices, shards(): lax.psum_scatter(jnp.concatenate([contract_rows(layer_one, grad_qkv), con...  356 us
    ppermute x3, waiting for transfers between devices, collect(): lax.ppermute(line, axis, [(d, (d - have) % ways) for d in range(ways)])  233 us
    all_gather x1, waiting for transfers between devices, shards(): lax.all_gather(part_feedforward, 'rep', axis=2, tiled=True)  97.3 us
    all_gather x1, waiting for transfers between devices, shards(): lax.all_gather(copies[0], 'fsdp', axis=0, tiled=True)  89.5 us
  transfers between devices with their start and end apart: 12, of which 9 were waited for; matrix products, arithmetic and copies ran while one was open for 11% of the time, Pallas kernels for 0%

profile of v1, /device:TPU:0, one launch (start us, length us, event | category | flops | bytes accessed | tf_op | source)
XLA Modules:
  0.0 2496.0 jit_solution(14411182239107334273)
XLA Ops:
  22.5 101.1 %collective-permute-done = bf16[160,5120]{1,0:T(8,128)(2,1)S(1)} collective-permute-done((bf16[160,5120]{1,0:T(8,128)(2,1)}, bf16[160,5120]{1,0:T(8,128)(2,1)S(1)}, u32[]{:S(2)}, u32[]{:S(2)}) %collective-permute-start) | collective-permute-done | bytes 1638432 | tf_op jit(solution)/shard_map/ppermute | solution.py:27
  131.3 131.8 %collective-permute-done.1 = bf16[320,5120]{1,0:T(8,128)(2,1)S(1)} collective-permute-done((bf16[320,5120]{1,0:T(8,128)(2,1)S(1)}, bf16[320,5120]{1,0:T(8,128)(2,1)S(1)}, u32[]{:S(2)}, u32[]{:S(2)}) %collective-permute-start.1) | collective-permute-done | bytes 3276832 | tf_op jit(solution)/shard_map/ppermute | solution.py:27
  271.8 439.8 %all-gather = bf16[8,160,12]{1,2,0:T(8,128)(2,1)S(1)} all-gather(bf16[1,160,12]{1,2,0:T(8,128)(2,1)S(1)} %copy.142), channel_id=1, replica_groups=mesh['rep'=4,'fsdp'=8] {'fsdp'}, dimensions={0}, use_global_device_ids=true | all-gather | bytes 34560 | tf_op jit(solution)/shard_map/all_gather | solution.py:105
  761.1 11.4 convert_reduce_fusion
  780.9 89.5 %all-gather.8.cloned.1.call-done = bf16[1280,5120]{1,0:T(8,128)(2,1)} async-done(((bf16[160,5120]{1,0:T(8,128)(2,1)}), bf16[1280,5120]{1,0:T(8,128)(2,1)}) %all-gather.8.cloned.1.call-update) | async-done | bytes 13107216 | tf_op jit(solution)/shard_map/all_gather | solution.py:152
  883.7 9.2 pad_maximum_fusion.1
  893.0 13.1 fusion.116
  906.1 12.3 fusion.111
  918.4 35.4 %pad_maximum_fusion = f32[1280,10240]{1,0:T(8,128)} fusion(f32[1280,5120]{1,0:T(8,128)} %fusion.111, f32[1280,5120]{1,0:T(8,128)} %fusion.116), kind=kLoop, calls=%fused_computation | loop fusion | flops 13107200 | bytes 104857600 | tf_op jit(solution)/shard_map/concatenate | solution.py:224
  953.8 355.7 %reduce-scatter.7.cloned.1.call-done = f32[160,5120]{1,0:T(8,128)} async-done(((f32[1280,5120]{1,0:T(8,128)}), f32[160,5120]{1,0:T(8,128)}) %reduce-scatter.7.cloned.1.call-update) | async-done | bytes 3276816 | tf_op jit(solution)/shard_map/reduce_scatter | solution.py:215
  1309.5 9.6 fusion.33
  1319.2 810.1 %reduce-scatter.9.cloned.1.call-done = f32[160,10240]{1,0:T(8,128)} async-done(((f32[1280,10240]{1,0:T(8,128)}), f32[160,10240]{1,0:T(8,128)}) %reduce-scatter.9.cloned.1.call-update) | async-done | bytes 6553616 | tf_op jit(solution)/shard_map/reduce_scatter | solution.py:223
  2129.3 18.2 fusion.15
  2165.9 12.6 fusion.117
  2178.5 22.4 reduce-scatter.15.cloned.1.call-done
  2211.0 13.2 fusion.54
  2224.2 42.8 %reduce-scatter.11.cloned.1.call-done = f32[12,160]{0,1:T(8,128)} async-done(((f32[12,1280]{0,1:T(8,128)}), f32[12,160]{0,1:T(8,128)}) %reduce-scatter.11.cloned.1.call-update) | async-done | bytes 7696 | tf_op jit(solution)/shard_map/reduce_scatter | solution.py:232
  2272.2 12.0 all-reduce
  2290.9 8.3 maximum_bitcast_fusion.2
  2299.2 35.5 %all-gather.10.cloned.1.call-done = f32[3,160,5120]{2,1,0:T(8,128)} async-done(((f32[3,160,1280]{2,1,0:T(8,128)}), f32[3,160,5120]{2,1,0:T(8,128)}) %all-gather.10.cloned.1.call-update) | async-done | bytes 9830416 | tf_op jit(solution)/shard_map/all_gather | solution.py:284
  2338.0 19.0 maximum_bitcast_fusion
  2363.2 97.3 %all-gather.12.cloned.1.call-done = f32[3,160,10240]{2,1,0:T(8,128)} async-done(((f32[3,160,2560]{2,1,0:T(8,128)}), f32[3,160,10240]{2,1,0:T(8,128)}) %all-gather.12.cloned.1.call-update) | async-done | bytes 19660816 | tf_op jit(solution)/shard_map/all_gather | solution.py:285
  2465.4 8.8 copy.187
  2474.2 15.0 copy.188
  (179 shorter events, 156.1 us)
Async XLA Ops:
  7.2 705.3 %copy-start = (s32[1,8]{1,0:T(1,128)S(1)}, s32[1,8]{1,0:T(1,128)}, u32[]{:S(2)}) copy-start(s32[1,8]{1,0:T(1,128)} %param.12) | copy-start | bytes 100
  7.2 747.5 %all-gather.6.cloned.1.call-start = ((), (), s32[]{:S(2)}) async-start(), calls=%async_computation.5 | async-start | bytes 29491200 | tf_op jit(solution)/shard_map/all_gather | solution.py:104
  12.2 858.2 %all-gather.8.cloned.1.call-start = ((), (), s32[]{:S(2)}) async-start(), calls=%async_computation.6 | async-start | bytes 14745600 | tf_op jit(solution)/shard_map/all_gather | solution.py:152
  16.4 107.2 %collective-permute-start = (bf16[160,5120]{1,0:T(8,128)(2,1)}, bf16[160,5120]{1,0:T(8,128)(2,1)S(1)}, u32[]{:S(2)}, u32[]{:S(2)}) collective-permute-start(bf16[160,5120]{1,0:T(8,128)(2,1)} %get-tuple-element.109), channel_id=1, source_target_pairs={{0,7},{1,0},{2,1},{3,2},{4,3},{5,4},{6,5},{7,6},{8,15},{9,8},{10,9... | collective-permute-start | bytes 4915208 | tf_op jit(solution)/shard_map/ppermute | solution.py:27
  22.4 1287.0 %reduce-scatter.7.cloned.1.call-start = ((), (), s32[]{:S(2)}) async-start(), calls=%async_computation.7 | async-start | bytes 29491200 | tf_op jit(solution)/shard_map/reduce_scatter | solution.py:215
  126.6 144.4 %copy-start.20 = (f32[2,12,160]{2,0,1:T(2,128)S(1)}, f32[2,12,160]{2,0,1:T(2,128)}, u32[]{:S(2)}) copy-start(f32[2,12,160]{2,0,1:T(2,128)} %param.16) | copy-start | bytes 46084
  126.6 136.5 %collective-permute-start.1 = (bf16[320,5120]{1,0:T(8,128)(2,1)S(1)}, bf16[320,5120]{1,0:T(8,128)(2,1)S(1)}, u32[]{:S(2)}, u32[]{:S(2)}) collective-permute-start(bf16[320,5120]{1,0:T(8,128)(2,1)S(1)} %pad_maximum_fusion.4), channel_id=1, source_target_pairs={{0,6},{1,7},{2,0},{3,1},{4,2},{5,3},{6,4},{7,5},{8,14},{9,15},{10,... | collective-permute-start | bytes 9830408 | tf_op jit(solution)/shard_map/ppermute | solution.py:27
  268.2 455.0 %collective-permute-start.2 = (bf16[640,5120]{1,0:T(8,128)(2,1)}, bf16[640,5120]{1,0:T(8,128)(2,1)}, u32[]{:S(2)}, u32[]{:S(2)}) collective-permute-start(bf16[640,5120]{1,0:T(8,128)(2,1)} %pad_maximum_fusion.2), channel_id=1, source_target_pairs={{0,4},{1,5},{2,6},{3,7},{4,0},{5,1},{6,2},{7,3},{8,12},{9,13},{10,... | collective-permute-start | bytes 19660808 | tf_op jit(solution)/shard_map/ppermute | solution.py:27
  271.7 451.6 %copy-start.13 = (f32[1,12,160]{1,2,0:T(8,128)}, f32[1,12,160]{1,2,0:T(8,128)S(1)}, u32[]{:S(2)}) copy-start(f32[1,12,160]{1,2,0:T(8,128)S(1)} %copy.171) | copy-start | bytes 23044
  754.4 138.6 %copy-start.7 = (f32[128,1280]{1,0:T(8,128)}, f32[128,1280]{1,0:T(8,128)S(1)}, u32[]{:S(2)}) copy-start(f32[128,1280]{1,0:T(8,128)S(1)} %get-tuple-element.140) | copy-start | bytes 1966084
  892.9 13.2 copy-start.17
  892.9 1236.3 %reduce-scatter.9.cloned.1.call-start = ((), (), s32[]{:S(2)}) async-start(), calls=%async_computation.8 | async-start | bytes 58982400 | tf_op jit(solution)/shard_map/reduce_scatter | solution.py:223
  893.0 13.1 copy-start.25
  953.8 1208.6 %reduce-scatter.13.cloned.1.call-start = ((), (), s32[]{:S(2)}) async-start(), calls=%async_computation.10 | async-start | bytes 2048000 | tf_op jit(solution)/shard_map/reduce_scatter | solution.py:243
  1319.1 881.8 %reduce-scatter.15.cloned.1.call-start = ((), (), s32[]{:S(2)}) async-start(), calls=%async_computation.12 | async-start | bytes 4096000 | tf_op jit(solution)/shard_map/reduce_scatter | solution.py:249
  2147.5 119.4 %reduce-scatter.11.cloned.1.call-start = ((), (), s32[]{:S(2)}) async-start(), calls=%async_computation.9 | async-start | bytes 737280 | tf_op jit(solution)/shard_map/reduce_scatter | solution.py:232
  2162.3 172.4 %all-gather.10.cloned.1.call-start = ((), (), s32[]{:S(2)}) async-start(), calls=%async_computation.11 | async-start | bytes 12288000 | tf_op jit(solution)/shard_map/all_gather | solution.py:284
  2165.8 294.7 %all-gather.12.cloned.1.call-start = ((), (), s32[]{:S(2)}) async-start(), calls=%async_computation.13 | async-start | bytes 24576000 | tf_op jit(solution)/shard_map/all_gather | solution.py:285
  2211.0 55.9 %copy-start.14 = (f32[1,12,160]{1,2,0:T(8,128)S(1)}, f32[1,12,160]{1,2,0:T(8,128)}, u32[]{:S(2)}) copy-start(f32[1,12,160]{1,2,0:T(8,128)} %copy-done.13) | copy-start | bytes 23044
  2211.0 79.8 %copy-start.4 = (f32[160,5120]{1,0:T(8,128)S(1)}, f32[160,5120]{1,0:T(8,128)}, u32[]{:S(2)}) copy-start(f32[160,5120]{1,0:T(8,128)} %reduce-scatter.7.cloned.1.call-done) | copy-start | bytes 9830404
  2338.0 19.0 slice-start
  2338.0 19.0 slice-start.1
  2338.0 19.7 copy-start.5
  2474.2 15.0 copy-start.1
  (16 other events, 72.0 us)
Sparse Core Ops, SparseCore 0:
  12.4 540.4 all-gather.5
  555.6 314.7 all-gather.7
  893.0 416.4 reduce-scatter.6
  1313.2 815.9 reduce-scatter.8
  2132.2 27.5 reduce-scatter.12
  2162.3 38.5 reduce-scatter.14
  2204.2 62.7 reduce-scatter.10
  2268.5 66.1 all-gather.9
  2336.3 124.1 all-gather.11
